TPU v7x, 32 devices: a whole 2x2x4 slice. The times are simulated.
32 devices in a mesh: seq: 4 (over y, core), shard: 2 (over x), replica: 4 (over z).
Axes of the slice: x: 2, y: 2, z: 4, core: 2. Of those that a mesh axis runs over, the one named last changes fastest.
Arguments:
- tokens: bfloat16 [8, 1024, 1536], P(('shard', 'replica'), 'seq'), may hold values from -6 to 6
- in_proj: bfloat16 [1536, 6448], P('shard'), may hold values from -0.15625 to 0.15625
- out_proj: bfloat16 [3072, 1536], P('shard'), may hold values from -0.109375 to 0.109375
- pre_gain: bfloat16 [1536], P('shard'), may hold values from 0.5 to 1.5
- conv_weight: bfloat16 [4, 3328], P(None, 'shard'), may hold values from -3 to 3
- conv_bias: bfloat16 [3328], P('shard'), may hold values from -3 to 3
- dt_bias: bfloat16 [48], P('shard'), may hold values from -6 to -3
- a_log: bfloat16 [48], P('shard'), may hold values from -3 to 1.5
- d_skip: bfloat16 [48], P('shard'), may hold values from 0.5 to 1.5
- norm_gain: bfloat16 [3072], P('shard'), may hold values from 0.5 to 1.5
- cotangent: bfloat16 [8, 1024, 1536], P(('shard', 'replica'), 'seq'), may hold values from -6 to 6
Outputs:
- block_out: float32 [8, 1024, 1536], P(('shard', 'replica'), 'seq')
- grad_tokens: float32 [8, 1024, 1536], P(('shard', 'replica'), 'seq')
- grad_in_proj: float32 [1536, 6448], P('shard')
- grad_out_proj: float32 [3072, 1536], P('shard')
- grad_pre_gain: float32 [1536], P('shard')
- grad_conv_weight: float32 [4, 3328], P(None, 'shard')
- grad_conv_bias: float32 [3328], P('shard')
- grad_dt_bias: float32 [48], P('shard')
- grad_a_log: float32 [48], P('shard')
- grad_d_skip: float32 [48], P('shard')
- grad_norm_gain: float32 [3072], P('shard')
All inputs are finite; a program needn't handle non-finite values.
Results may differ from a plain program's by a relative error of at most 0.0059.
Values may be sent and summed in bfloat16 or wider, within the bound.
A program may use at most 320 MiB of HBM per device.

v0:
```python
import jax
import jax.numpy as jnp
from jax import lax
from jax.sharding import PartitionSpec as P

D = 1536
H = 48
P_SIZE = 64
NSTATE = 128
CONVK = 4
INNER = 3072
XBC = 3328
PROJ = 6448


epsilon = 1e-05
highest = lax.Precision.HIGHEST


def passed_along(block, axis, distance):
    devices = range(lax.axis_size(axis))
    route = [(i - distance, i) for i in devices if i - distance in devices]
    return lax.ppermute(block, axis, route)


def entering(value, axis, join, neutral, backward):
    count, mine = (lax.axis_size(axis), lax.axis_index(axis))
    pieces = jax.tree.map(lambda part: lax.all_gather(part, axis), value)
    if backward:
        pieces = jax.tree.map(lambda part: part[::-1], pieces)
        mine = count - 1 - mine
    total = jax.tree.map(
        lambda part, zero: jnp.full_like(part, 0) + jnp.asarray(zero, part.dtype), value, neutral
    )

    def turn(position, total):
        longer = join(total, jax.tree.map(lambda part: part[position], pieces))
        return jax.tree.map(lambda new, old: jnp.where(position < mine, new, old), longer, total)

    return lax.fori_loop(0, count - 1, turn, total)


def convolve(extended, conv_weight, conv_bias, seq_length):
    total = conv_bias
    for offset in range(CONVK):
        total = total + conv_weight[offset] * extended[:, offset : offset + seq_length]
    return total


def prepare(projected, halo_rows, conv_weight, conv_bias, dt_bias, a_log):
    seq_count, seq_length = (projected.shape[0], projected.shape[1])
    gate_z = projected[..., :INNER]
    extended = jnp.concatenate([halo_rows, projected[..., INNER : INNER + XBC]], axis=1)
    activated = jax.nn.silu(convolve(extended, conv_weight, conv_bias, seq_length))
    values = activated[..., :INNER].reshape(seq_count, seq_length, H, P_SIZE)
    b_state = activated[..., INNER : INNER + NSTATE]
    c_state = activated[..., INNER + NSTATE :]
    step_size = jax.nn.softplus(projected[..., INNER + XBC :] + dt_bias)
    log_decay = -step_size * jnp.exp(a_log)
    return (values, b_state, c_state, step_size, log_decay, gate_z)


def span_local(values, b_state, c_state, step_size, log_decay):
    seq_length = values.shape[1]
    cumulative = jnp.cumsum(log_decay, axis=1)
    inner_bc = jnp.einsum("stn,sun->stu", c_state, b_state, precision=highest)
    lower = jnp.arange(seq_length)[:, None] >= jnp.arange(seq_length)[None, :]
    differ = cumulative[:, :, None, :] - cumulative[:, None, :, :]
    kernel = (
        jnp.exp(jnp.where(lower[None, :, :, None], differ, -10000.0))
        * inner_bc[..., None]
        * step_size[:, None, :, :]
    )
    y_intra = jnp.einsum("stuh,suhp->sthp", kernel, values, precision=highest)
    decays = jnp.exp(cumulative)
    a_total = decays[:, -1, :]
    tail_weight = jnp.exp(cumulative[:, -1:, :] - cumulative) * step_size
    h_local = jnp.einsum("suh,suhp,sun->shpn", tail_weight, values, b_state, precision=highest)
    return (y_intra, decays, a_total, h_local)


def finish(y_intra, decays, c_state, h_enter, values, gate_z, d_skip, norm_gain):
    seq_count, seq_length = (values.shape[0], values.shape[1])
    y_inter = decays[..., None] * jnp.einsum("stn,shpn->sthp", c_state, h_enter, precision=highest)
    y_core = (y_intra + y_inter + d_skip[:, None] * values).reshape(seq_count, seq_length, INNER)
    gated = y_core * jax.nn.silu(gate_z)
    inverse = lax.rsqrt(jnp.mean(gated * gated, axis=-1, keepdims=True) + epsilon)
    return gated * inverse * norm_gain


def compose(earlier, later):
    return (earlier[0] * later[0], later[0][:, :, None, None] * earlier[1] + later[1])


def body(
    tokens,
    in_proj,
    out_proj,
    pre_gain,
    conv_weight,
    conv_bias,
    dt_bias,
    a_log,
    d_skip,
    norm_gain,
    cotangent,
):
    gathered = (
        lax.all_gather(in_proj, "shard", axis=0, tiled=True),
        lax.all_gather(out_proj, "shard", axis=0, tiled=True),
        lax.all_gather(pre_gain, "shard", axis=0, tiled=True),
        lax.all_gather(conv_weight, "shard", axis=1, tiled=True),
        lax.all_gather(conv_bias, "shard", axis=0, tiled=True),
        lax.all_gather(dt_bias, "shard", axis=0, tiled=True),
        lax.all_gather(a_log, "shard", axis=0, tiled=True),
        lax.all_gather(d_skip, "shard", axis=0, tiled=True),
        lax.all_gather(norm_gain, "shard", axis=0, tiled=True),
    )
    in_whole, out_whole = (gathered[0], gathered[1])
    small_params = tuple((piece.astype(jnp.float32) for piece in gathered[2:]))
    pre_whole = small_params[0]
    seq_count, seq_length = (tokens.shape[0], tokens.shape[1])
    rows_total = seq_count * seq_length
    tokens_wide = tokens.astype(jnp.float32)
    inverse = lax.rsqrt(jnp.mean(tokens_wide * tokens_wide, axis=-1, keepdims=True) + epsilon)
    normed = (tokens_wide * inverse * pre_whole).astype(jnp.bfloat16).reshape(rows_total, D)
    projected = jnp.dot(normed, in_whole, preferred_element_type=jnp.float32).reshape(
        seq_count, seq_length, PROJ
    )
    halo_rows = passed_along(
        projected[:, seq_length - (CONVK - 1) :, INNER : INNER + XBC], "seq", 1
    )
    prepared, prepare_back = jax.vjp(prepare, projected, halo_rows, *small_params[1:5])
    values, b_state, c_state, step_size, log_decay, gate_z = prepared
    span_out, span_back = jax.vjp(span_local, values, b_state, c_state, step_size, log_decay)
    y_intra, decays, a_total, h_local = span_out
    identity = (jnp.ones_like(a_total), jnp.zeros_like(h_local))
    h_enter = entering((a_total, h_local), "seq", compose, identity, False)[1]
    mixed, finish_back = jax.vjp(
        finish, y_intra, decays, c_state, h_enter, values, gate_z, small_params[5], small_params[6]
    )
    mixed_low = mixed.astype(jnp.bfloat16).reshape(rows_total, INNER)
    branch = jnp.dot(mixed_low, out_whole, preferred_element_type=jnp.float32)
    block_out = tokens_wide + branch.reshape(seq_count, seq_length, D)
    in_again, out_again = (
        lax.all_gather(in_proj, "shard", axis=0, tiled=True),
        lax.all_gather(out_proj, "shard", axis=0, tiled=True),
    )
    cot_rows = cotangent.reshape(rows_total, D)
    grad_out = jnp.dot(mixed_low.T, cot_rows, preferred_element_type=jnp.float32)
    d_mixed = jnp.dot(cot_rows, out_again.T, preferred_element_type=jnp.float32).reshape(
        seq_count, seq_length, INNER
    )
    d_intra, d_decays, d_cstate, d_enter, d_values, d_gate, grad_skip, grad_norm = finish_back(
        d_mixed
    )
    d_exit = entering((a_total, d_enter), "seq", compose, identity, True)[1]
    d_total = jnp.sum(d_exit * h_enter, axis=(2, 3))
    d_values_scan, d_bstate, d_cstate_scan, d_step, d_log = span_back(
        (d_intra, d_decays, d_total, d_exit)
    )
    d_projected, d_halo, grad_conv_weight, grad_conv_bias, grad_dt_bias, grad_a_log = prepare_back(
        (d_values + d_values_scan, d_bstate, d_cstate + d_cstate_scan, d_step, d_log, d_gate)
    )
    returned = passed_along(d_halo, "seq", -1)
    d_projected = d_projected.at[:, seq_length - (CONVK - 1) :, INNER : INNER + XBC].add(returned)
    d_proj_low = d_projected.astype(jnp.bfloat16).reshape(rows_total, PROJ)
    grad_in = jnp.dot(normed.T, d_proj_low, preferred_element_type=jnp.float32)
    d_normed = jnp.dot(d_proj_low, in_again.T, preferred_element_type=jnp.float32).reshape(
        seq_count, seq_length, D
    )
    grad_pre = jnp.sum((d_normed * tokens_wide * inverse).reshape(rows_total, D), axis=0)
    d_scaled = d_normed * pre_whole
    d_tokens = (
        cotangent.astype(jnp.float32)
        + inverse * d_scaled
        - tokens_wide
        * (inverse * inverse * inverse)
        * jnp.mean(d_scaled * tokens_wide, axis=-1, keepdims=True)
    )
    owned = (
        lax.psum_scatter(grad_in, "shard", scatter_dimension=0, tiled=True),
        lax.psum_scatter(grad_out, "shard", scatter_dimension=0, tiled=True),
        lax.psum_scatter(grad_pre, "shard", scatter_dimension=0, tiled=True),
        lax.psum_scatter(grad_conv_weight, "shard", scatter_dimension=1, tiled=True),
        lax.psum_scatter(grad_conv_bias, "shard", scatter_dimension=0, tiled=True),
        lax.psum_scatter(grad_dt_bias, "shard", scatter_dimension=0, tiled=True),
        lax.psum_scatter(grad_a_log, "shard", scatter_dimension=0, tiled=True),
        lax.psum_scatter(grad_skip, "shard", scatter_dimension=0, tiled=True),
        lax.psum_scatter(grad_norm, "shard", scatter_dimension=0, tiled=True),
    )
    summed = lax.psum(
        (owned[0], owned[1], owned[2], owned[3], owned[4], owned[5], owned[6], owned[7], owned[8]),
        ("seq", "replica"),
    )
    return (
        block_out,
        d_tokens,
        summed[0],
        summed[1],
        summed[2],
        summed[3],
        summed[4],
        summed[5],
        summed[6],
        summed[7],
        summed[8],
    )


def solution(mesh):
    in_specs = (
        P(("shard", "replica"), "seq", None),
        P("shard", None),
        P("shard", None),
        P("shard"),
        P(None, "shard"),
        P("shard"),
        P("shard"),
        P("shard"),
        P("shard"),
        P("shard"),
        P(("shard", "replica"), "seq", None),
    )
    out_specs = (
        P(("shard", "replica"), "seq", None),
        P(("shard", "replica"), "seq", None),
        P("shard", None),
        P("shard", None),
        P("shard"),
        P(None, "shard"),
        P("shard"),
        P("shard"),
        P("shard"),
        P("shard"),
        P("shard"),
    )
    return jax.shard_map(body, mesh=mesh, in_specs=in_specs, out_specs=out_specs, check_vma=False)
```

profile of v0, /device:TPU:0, one launch (start us, length us, event | category | flops | bytes accessed | tf_op | source)
XLA Modules:
  0.0 1741.9 jit_solution(9450739963692779270)
XLA Ops:
  10.1 6.3 all-reduce.28
  31.9 215.0 %all-gather.10.cloned.1.call-done = bf16[1536,6448]{0,1:T(8,128)(2,1)} async-done(((bf16[768,6448]{0,1:T(8,128)(2,1)}), bf16[1536,6448]{0,1:T(8,128)(2,1)}) %all-gather.10.cloned.1.call-update) | async-done | bytes 19808272 | tf_op jit(solution)/shard_map/all_gather | solution.py:109
  247.0 10.1 convolution_bitcast_fusion
  271.5 10.0 fusion.23
  300.6 16.6 fusion.4
  317.2 17.5 %all-gather.14.cloned.1.call-done = f32[192,64,128]{2,1,0:T(8,128)} async-done(((f32[48,64,128]{2,1,0:T(8,128)}), f32[192,64,128]{2,1,0:T(8,128)}) %all-gather.14.cloned.1.call-update) | async-done | bytes 6291472 | tf_op jit(solution)/shard_map/all_gather | solution.py:28
  354.8 99.5 %all-gather.12.cloned.1.call-done = bf16[3072,1536]{1,0:T(8,128)(2,1)} async-done(((bf16[1536,1536]{1,0:T(8,128)(2,1)}), bf16[3072,1536]{1,0:T(8,128)(2,1)}) %all-gather.12.cloned.1.call-update) | async-done | bytes 9437200 | tf_op jit(solution)/shard_map/all_gather | solution.py:110
  454.3 8.5 fusion.32
  462.8 6.4 multiply_reduce_fusion.5
  476.3 12.9 fusion.76
  490.0 21.5 %fusion.6 = (f32[256,48]{0,1:T(8,128)}, f32[256,48]{0,1:T(8,128)}, f32[256,48]{0,1:T(8,128)}, f32[256,256]{1,0:T(8,128)S(1)}) fusion(f32[256,48]{0,1:T(8,128)} %get-tuple-element.350, f32[256,256]{1,0:T(8,128)} %copy-done.30, f32[256,48]{0,1:T(8,128)S(1)} %copy-done.44, pred[256,256]{1,0:T(8,128)(4,1)} %copy-done.38, f32[48,64,256]{2,1,0:T(8,128)} %bitcast.319, ...), kind=kOutput, calls=%fused_computation.17 | convolution fusion | flops 2456711168 | bytes 7127040 | tf_op jit(solution)/shard_map/transpose(jvp(stuh,suhp->sthp))/dot_general | solution.py:74
  522.8 6.5 rev.7
  551.2 14.7 fusion.30
  566.0 12.1 multiply_reduce_fusion.3
  604.9 10.8 scatter-add.4
  615.7 19.1 %fusion.24 = f32[1536,6448]{0,1:T(8,128)} fusion(f32[1,256,6448]{1,2,0:T(8,128)} %scatter-add.4, bf16[1,256,1536]{2,1,0:T(8,128)(2,1)S(1)} %copy-done.17, f32[1536]{0:T(1024)S(1)} %copy-done.36, f32[256]{0:T(256)S(1)} %copy-done.49), kind=kOutput, calls=%fused_computation.57 | convolution fusion | flops 5074137088 | bytes 47012864 | tf_op jit(solution)/shard_map/dot_general | solution.py:168
  637.5 99.7 %reduce-scatter.8.cloned.1.call-done = f32[1536,1536]{1,0:T(8,128)} async-done(((f32[3072,1536]{1,0:T(8,128)}), f32[1536,1536]{1,0:T(8,128)}) %reduce-scatter.8.cloned.1.call-update) | async-done | bytes 9437200 | tf_op jit(solution)/shard_map/reduce_scatter | solution.py:183
  737.3 436.5 %reduce-scatter.6.cloned.1.call-done = f32[768,6448]{0,1:T(8,128)} async-done(((f32[1536,6448]{0,1:T(8,128)}), f32[768,6448]{0,1:T(8,128)}) %reduce-scatter.6.cloned.1.call-update) | async-done | bytes 19808272 | tf_op jit(solution)/shard_map/reduce_scatter | solution.py:182
  1176.6 8.6 convert_add_fusion
  1185.3 11.1 fusion.50
  1196.4 7.9 all-reduce.27
  1209.5 65.0 %all-reduce.25 = (f32[768]{0:T(1024)}, f32[4,1664]{1,0:T(4,128)}, f32[1664]{0:T(1024)}, f32[24]{0:T(128)}, f32[24]{0:T(128)}, /*index=5*/f32[24]{0:T(128)}, f32[1536]{0:T(1024)}) all-reduce(f32[768]{0:T(1024)S(1)} %dynamic-slice.13, f32[4,1664]{1,0:T(4,128)S(1)} %copy.130, ...), channel_id=1, replica_groups=mesh['seq'=4,'shard'=2,'replica'=4] {'seq','replica'}, use_global_device_ids=true, to_apply=%region_25.26 | all-reduce | flops 10696 | bytes 85568 | tf_op jit(solution)/shard_map/psum | solution.py:192
  1274.5 440.1 %all-reduce.31.cloned.1.call-done = (f32[768,6448]{0,1:T(8,128)}, f32[1536,1536]{1,0:T(8,128)}) async-done(((f32[768,6448]{0,1:T(8,128)}, f32[1536,1536]{1,0:T(8,128)}), (f32[768,6448]{0,1:T(8,128)}, f32[1536,1536]{1,0:T(8,128)})) %all-reduce.31.cloned.1.call-update) | async-done | bytes 29245456 | tf_op jit(solution)/shard_map/psum | solution.py:192
  1714.6 15.3 copy.167
  (291 shorter events, 162.4 us)
Async XLA Ops:
  7.2 18.7 %copy-start.50 = (bf16[4,1664]{1,0:T(4,128)(2,1)S(1)}, bf16[4,1664]{1,0:T(4,128)(2,1)}, u32[]{:S(2)}) copy-start(bf16[4,1664]{1,0:T(4,128)(2,1)} %param.21) | copy-start | bytes 39940
  7.3 23.8 %copy-start.16 = (bf16[1,256,1536]{2,1,0:T(8,128)(2,1)S(1)}, bf16[1,256,1536]{2,1,0:T(8,128)(2,1)}, u32[]{:S(2)}) copy-start(bf16[1,256,1536]{2,1,0:T(8,128)(2,1)} %param.17) | copy-start | bytes 2359300
  7.3 239.7 %all-gather.10.cloned.1.call-start = ((), (), s32[]{:S(2)}) async-start(), calls=%async_computation.3 | async-start | bytes 29712384 | tf_op jit(solution)/shard_map/all_gather | solution.py:109
  8.0 326.7 %all-gather.14.cloned.1.call-start = ((), (), s32[]{:S(2)}) async-start(), calls=%async_computation.7 | async-start | bytes 7864320 | tf_op jit(solution)/shard_map/all_gather | solution.py:28
  16.4 240.6 %copy-start.67 = (bf16[48]{0:T(256)(128)(2,1)}, bf16[48]{0:T(256)(128)(2,1)S(1)}, u32[]{:S(2)}) copy-start(bf16[48]{0:T(256)(128)(2,1)S(1)} %get-tuple-element.332) | copy-start | bytes 292
  16.4 248.8 %copy-start.52 = (f32[48]{0:T(128)}, f32[48]{0:T(128)S(1)}, u32[]{:S(2)}) copy-start(f32[48]{0:T(128)S(1)} %convert_element_type.41) | copy-start | bytes 580
  20.9 226.1 %copy-start.35 = (f32[1536]{0:T(1024)}, f32[1536]{0:T(1024)S(1)}, u32[]{:S(2)}) copy-start(f32[1536]{0:T(1024)S(1)} %reshape.589) | copy-start | bytes 18436
  31.3 226.2 %copy-start.59 = (f32[48]{0:T(128)}, f32[48]{0:T(128)S(1)}, u32[]{:S(2)}) copy-start(f32[48]{0:T(128)S(1)} %convert_exponential_fusion) | copy-start | bytes 580
  31.9 215.0 %copy-start.48 = (f32[256]{0:T(256)}, f32[256]{0:T(256)S(1)}, u32[]{:S(2)}) copy-start(f32[256]{0:T(256)S(1)} %get-tuple-element.357) | copy-start | bytes 3076
  263.0 5.9 collective-permute-start
  288.1 166.2 %all-gather.12.cloned.1.call-start = ((), (), s32[]{:S(2)}) async-start(), calls=%async_computation.4 | async-start | bytes 14155776 | tf_op jit(solution)/shard_map/all_gather | solution.py:110
  288.8 233.9 %all-gather.16.cloned.1.call-start = ((), (), s32[]{:S(2)}) async-start(), calls=%async_computation.8 | async-start | bytes 7864320 | tf_op jit(solution)/shard_map/all_gather | solution.py:28
  293.4 23.8 %copy-start.38 = (pred[256,256]{1,0:T(8,128)(4,1)}, pred[256,256]{1,0:T(8,128)(4,1)S(1)}, u32[]{:S(2)}) copy-start(pred[256,256]{1,0:T(8,128)(4,1)S(1)} %iota_compare_fusion) | copy-start | bytes 196612
  299.1 18.1 %copy-start.43 = (f32[256,48]{0,1:T(8,128)}, f32[256,48]{0,1:T(8,128)S(1)}, u32[]{:S(2)}) copy-start(f32[256,48]{0,1:T(8,128)S(1)} %fusion.109) | copy-start | bytes 147460
  348.8 105.5 %copy-start.19 = (bf16[1,256,1536]{2,1,0:T(8,128)(2,1)S(1)}, bf16[1,256,1536]{2,1,0:T(8,128)(2,1)}, u32[]{:S(2)}) copy-start(bf16[1,256,1536]{2,1,0:T(8,128)(2,1)} %param.27) | copy-start | bytes 2359300
  476.3 261.0 %reduce-scatter.8.cloned.1.call-start = ((), (), s32[]{:S(2)}) async-start(), calls=%async_computation.6 | async-start | bytes 28311552 | tf_op jit(solution)/shard_map/reduce_scatter | solution.py:183
  489.2 684.5 %reduce-scatter.6.cloned.1.call-start = ((), (), s32[]{:S(2)}) async-start(), calls=%async_computation.5 | async-start | bytes 59424768 | tf_op jit(solution)/shard_map/reduce_scatter | solution.py:182
  490.0 23.6 %copy-start.11 = (f32[1,256,3072]{1,2,0:T(8,128)S(1)}, f32[1,256,3072]{1,2,0:T(8,128)}, u32[]{:S(2)}) copy-start(f32[1,256,3072]{1,2,0:T(8,128)} %copy-done.10) | copy-start | bytes 9437188
  490.0 28.4 %copy-start.15 = (f32[256,48,64]{0,2,1:T(8,128)S(1)}, f32[256,48,64]{0,2,1:T(8,128)}, u32[]{:S(2)}) copy-start(f32[256,48,64]{0,2,1:T(8,128)} %copy-done.14) | copy-start | bytes 9437188
  546.3 19.7 %slice-start.2 = ((s8[6602752]{0:T(1024)(128)(4,1)}), s8[4194304]{0:T(1024)(128)(4,1)S(1)}, s32[]{:S(2)}) async-start(s8[6602752]{0:T(1024)(128)(4,1)} %bitcast.317), calls=%async_computation.13 | async-start | bytes 8388608
  592.2 7.5 collective-permute-start.1
  634.9 573.2 %reduce-scatter.10.cloned.1.call-start = ((), (), s32[]{:S(2)}) async-start(), calls=%async_computation.9 | async-start | bytes 2555904
  637.5 1077.1 %all-reduce.31.cloned.1.call-start = ((), (), s32[]{:S(2)}) async-start(), calls=%async_computation.10 | async-start | bytes 58490880 | tf_op jit(solution)/shard_map/psum | solution.py:192
  1185.3 19.5 %copy-start.56 = (f32[256]{0:T(256)S(1)}, f32[256]{0:T(256)}, u32[]{:S(2)}) copy-start(f32[256]{0:T(256)} %get-tuple-element.356) | copy-start | bytes 3076
  (60 other events, 443.2 us)
Sparse Core Ops, SparseCore 0:
  9.6 237.2 all-gather.9
  288.2 46.4 all-gather.13
  336.3 117.9 all-gather.11
  476.4 46.3 all-gather.15
  525.5 211.7 reduce-scatter.7
  739.4 434.2 reduce-scatter.5
  1176.0 28.1 reduce-scatter.9
  1208.5 506.0 all-reduce.30
where the time goes:
time: 1750 us; the launch traced here: 1740 us
  waiting for transfers between devices  1310 us (75%)
  matrix products  153 us (9%)
  blocking collectives  102 us (6%)
  other arithmetic  82.2 us (5%)
  local copies, waits for them, and re-layouts  68.4 us (4%)
  between operations  18.5 us (1%)
    psum x1, waiting for transfers between devices, body(): lax.psum((owned[0], owned[1], owned[2], owned[3], owned[4], owned[5], own...  440 us
    reduce_scatter x1, waiting for transfers between devices, body(): lax.psum_scatter(grad_in, 'shard', scatter_dimension=0, tiled=True)  436 us
    all_gather x1, waiting for transfers between devices, body(): lax.all_gather(in_proj, 'shard', axis=0, tiled=True)  215 us
    reduce_scatter x1, waiting for transfers between devices, body(): lax.psum_scatter(grad_out, 'shard', scatter_dimension=0, tiled=True)  99.7 us
    all_gather x1, waiting for transfers between devices, body(): lax.all_gather(out_proj, 'shard', axis=0, tiled=True)  99.5 us
    psum x1, blocking collectives, body(): lax.psum((owned[0], owned[1], owned[2], owned[3], owned[4], owned[5], own...  65 us
    dot_general x3, matrix products, span_local(): y_intra = jnp.einsum('stuh,suhp->sthp', kernel, values, precision=highest)  52.8 us
  transfers between devices with their start and end apart: 10, of which 7 were waited for; matrix products, arithmetic and copies ran while one was open for 13% of the time, Pallas kernels for 0%

commit v1 on v0

--- a/solution.py
+++ b/solution.py
@@ -207,6 +207,231 @@
         summed[8],
     )
 
+f32, bf16 = jnp.float32, jnp.bfloat16
+
+
+def chunk_step(state, piece):
+    values, b_state, c_state, step_size, log_decay = piece
+    y_intra, decays, a_total, h_local = span_local(values, b_state, c_state, step_size, log_decay)
+    y_inter = decays[..., None] * jnp.einsum("stn,shpn->sthp", c_state, state, precision=highest)
+    return a_total[:, :, None, None] * state + h_local, y_intra + y_inter
+
+
+def core(xv, bc, dt_raw, conv_v, conv_bc, bias_v, bias_bc, dt_bias, a_log, d_skip):
+    seqs, length = xv.shape[:2]
+    heads = dt_raw.shape[-1]
+
+    def act(raw, weight, bias):
+        extended = jnp.pad(raw, ((0, 0), (CONVK - 1, 0), (0, 0)))
+        return jax.nn.silu(convolve(extended, weight, bias, length))
+
+    values = act(xv, conv_v, bias_v).reshape(seqs, length, heads, P_SIZE)
+    state = act(bc, conv_bc, bias_bc)
+    step_size = jax.nn.softplus(dt_raw + dt_bias)
+    log_decay = -step_size * jnp.exp(a_log)
+    span = min(256, length)
+    pieces = tuple(
+        jnp.moveaxis(p.reshape((seqs, length // span, span) + p.shape[2:]), 1, 0)
+        for p in (values, state[..., :NSTATE], state[..., NSTATE:], step_size, log_decay)
+    )
+    start = jnp.zeros((seqs, heads, P_SIZE, NSTATE), f32)
+    _, y = lax.scan(chunk_step, start, pieces, unroll=True)
+    y = jnp.moveaxis(y, 0, 1).reshape(seqs, length, heads, P_SIZE)
+    return (y + d_skip[:, None] * values).reshape(seqs, length, heads * P_SIZE)
+
+
+TP = ("shard", "seq")
+
+
+def split_body(
+    tokens,
+    in_proj,
+    out_proj,
+    pre_gain,
+    conv_weight,
+    conv_bias,
+    dt_bias,
+    a_log,
+    d_skip,
+    norm_gain,
+    cotangent,
+):
+    n_shard, n_seq, n_rep = (lax.axis_size(a) for a in ("shard", "seq", "replica"))
+    x, s = lax.axis_index("shard"), lax.axis_index("seq")
+    ranks = n_shard * n_seq
+    me = x * n_seq + s
+    heads = H // ranks
+    wide = INNER // ranks
+    slim = 2 * NSTATE // ranks
+    tok = tokens.reshape(-1, D)
+    own_rows = tok.shape[0]
+    seqs, length = n_shard, n_seq * own_rows
+    rows = seqs * length
+    kown = in_proj.shape[0]
+
+    tok_all = lax.all_gather(tok, TP, axis=0, tiled=True)
+    cot_all = lax.all_gather(cotangent.reshape(-1, D), TP, axis=0, tiled=True)
+
+    def columns(rank):
+        cut = lambda at, n: lax.dynamic_slice_in_dim(in_proj, at, n, 1)
+        return jnp.concatenate(
+            [
+                cut(rank * wide, wide),
+                cut(INNER + rank * wide, wide),
+                in_proj[:, 2 * INNER : INNER + XBC],
+                cut(INNER + XBC + rank * heads, heads),
+            ],
+            axis=1,
+        )
+
+    blocks = []
+    for hop in range(n_shard):
+        to = (x + hop) % n_shard
+        piece = columns(to * n_seq + s)
+        if hop:
+            piece = lax.ppermute(piece, "shard", [(i, (i + hop) % n_shard) for i in range(n_shard)])
+        blocks.append(piece)
+    stack = jnp.stack(blocks)
+    order = (x - jnp.arange(n_shard)) % n_shard
+    w_own = stack[order].reshape(n_shard * kown, -1)
+    small = jnp.concatenate(
+        [
+            p.reshape(-1)
+            for p in (pre_gain, conv_weight, conv_bias, dt_bias, a_log, d_skip, norm_gain)
+        ]
+    )
+    small = lax.all_gather(small, "shard", axis=0).astype(f32)
+    sizes = (pre_gain.size, conv_weight.size, conv_bias.size, dt_bias.size, a_log.size, d_skip.size)
+    at = [0]
+    for n in sizes:
+        at.append(at[-1] + n)
+    pre_whole = small[:, at[0] : at[1]].reshape(-1)
+    cw = small[:, at[1] : at[2]].reshape(n_shard, CONVK, -1)
+    cw = jnp.moveaxis(cw, 0, 1).reshape(CONVK, XBC)
+    cb = small[:, at[2] : at[3]].reshape(-1)
+    own = lambda full, n: lax.dynamic_slice_in_dim(full.reshape(-1), me * n, n, 0)
+    dtb = own(small[:, at[3] : at[4]], heads)
+    alog = own(small[:, at[4] : at[5]], heads)
+    skip = own(small[:, at[5] : at[6]], heads)
+    gain = own(small[:, at[6] :], wide)
+    conv_v = lax.dynamic_slice_in_dim(cw, me * wide, wide, 1)
+    bias_v = lax.dynamic_slice_in_dim(cb, me * wide, wide, 0)
+    conv_bc, bias_bc = cw[:, INNER:], cb[INNER:]
+    out_own = lax.dynamic_slice_in_dim(out_proj, s * wide, wide, 0)
+
+    wide_all = tok_all.astype(f32)
+    inverse_all = lax.rsqrt(jnp.mean(wide_all * wide_all, axis=-1, keepdims=True) + epsilon)
+    normed = (wide_all * inverse_all * pre_whole).astype(bf16)
+    projected = jnp.dot(normed, w_own, preferred_element_type=f32).reshape(seqs, length, -1)
+    gate = projected[..., :wide]
+    xv = projected[..., wide : 2 * wide]
+    bc = projected[..., 2 * wide : 2 * wide + 2 * NSTATE]
+    dt_raw = projected[..., 2 * wide + 2 * NSTATE :]
+    y_core, core_back = jax.vjp(
+        core, xv, bc, dt_raw, conv_v, conv_bc, bias_v, bias_bc, dtb, alog, skip
+    )
+    sig = jax.nn.sigmoid(gate)
+    silu = gate * sig
+    gated = y_core * silu
+    total = lax.psum(jnp.sum(gated * gated, axis=-1), TP)
+    inv = lax.rsqrt(total / INNER + epsilon)[..., None]
+    mixed = (gated * inv * gain).astype(bf16).reshape(rows, wide)
+    branch = jnp.dot(mixed, out_own, preferred_element_type=f32).astype(bf16)
+    branch = lax.psum_scatter(branch, TP, scatter_dimension=0, tiled=True)
+    tok_wide = tok.astype(f32)
+    block_out = tok_wide + branch.astype(f32)
+
+    g_out = jnp.dot(mixed.T, cot_all, preferred_element_type=f32).astype(bf16)
+    d_mixed = jnp.dot(cot_all, out_own.T, preferred_element_type=f32).reshape(seqs, length, wide)
+    grad_gain = jnp.sum(d_mixed * gated * inv, axis=(0, 1))
+    u = d_mixed * gain
+    dot = lax.psum(jnp.sum(u * gated, axis=-1), TP)[..., None]
+    d_gated = inv * u - gated * (inv * inv * inv) * (dot / INNER)
+    d_y = d_gated * silu
+    d_gate = d_gated * y_core * (sig * (1.0 + gate * (1.0 - sig)))
+    d_xv, d_bc, d_dt, g_cv, g_cbc, g_bv, g_bbc, g_dtb, g_alog, g_skip = core_back(d_y)
+    d_bc = lax.psum_scatter(d_bc.reshape(rows, -1), TP, scatter_dimension=1, tiled=True)
+    d_own = jnp.concatenate(
+        [
+            d_gate.reshape(rows, wide).astype(bf16),
+            d_xv.reshape(rows, wide).astype(bf16),
+            d_bc.astype(bf16),
+            d_dt.reshape(rows, heads).astype(bf16),
+        ],
+        axis=1,
+    )
+    w_back = jnp.concatenate(
+        [
+            w_own[:, : 2 * wide],
+            lax.dynamic_slice_in_dim(w_own, 2 * wide + me * slim, slim, 1),
+            w_own[:, 2 * wide + 2 * NSTATE :],
+        ],
+        axis=1,
+    )
+    d_normed = jnp.dot(d_own, w_back.T, preferred_element_type=f32).astype(bf16)
+    d_normed = lax.psum_scatter(d_normed, TP, scatter_dimension=0, tiled=True).astype(f32)
+    g_in = jnp.dot(normed.T, d_own, preferred_element_type=f32).astype(bf16)
+
+    inverse = lax.rsqrt(jnp.mean(tok_wide * tok_wide, axis=-1, keepdims=True) + epsilon)
+    grad_pre = jnp.sum(d_normed * tok_wide * inverse, axis=0)
+    d_scaled = d_normed * pre_whole
+    grad_tokens = (
+        cotangent.reshape(-1, D).astype(f32)
+        + inverse * d_scaled
+        - tok_wide
+        * (inverse * inverse * inverse)
+        * jnp.mean(d_scaled * tok_wide, axis=-1, keepdims=True)
+    )
+
+    every = ("seq", "shard", "replica")
+    place = lambda part, n, total_size: lax.dynamic_update_slice_in_dim(
+        jnp.zeros(part.shape[:-1] + (total_size,), f32), part, n, part.ndim - 1
+    )
+    grad_cw = jnp.concatenate([place(g_cv, me * wide, INNER), g_cbc], axis=1)
+    grad_cb = jnp.concatenate([place(g_bv, me * wide, INNER), g_bbc])
+    smalls = lax.psum(
+        (
+            grad_pre,
+            grad_cw,
+            grad_cb,
+            place(g_dtb, me * heads, H),
+            place(g_alog, me * heads, H),
+            place(g_skip, me * heads, H),
+            place(grad_gain, me * wide, INNER),
+        ),
+        every,
+    )
+    mine = lambda full: lax.dynamic_slice_in_dim(
+        full, x * (full.shape[-1] // n_shard), full.shape[-1] // n_shard, full.ndim - 1
+    )
+    smalls = [mine(v) for v in smalls]
+
+    g_out = lax.psum_scatter(g_out, "replica", scatter_dimension=0, tiled=True)
+    g_out = lax.all_gather(g_out, ("seq", "replica"), axis=0, tiled=True).astype(f32)
+    g_in = g_in.reshape(n_shard, kown, -1)
+    g_in = lax.psum_scatter(g_in, "replica", scatter_dimension=1, tiled=True)
+    parts = []
+    for hop in range(n_shard):
+        piece = g_in[(x + hop) % n_shard]
+        if hop:
+            piece = lax.ppermute(piece, "shard", [(i, (i + hop) % n_shard) for i in range(n_shard)])
+        parts.append(piece)
+    g_in = jnp.stack(parts)[order]
+    g_in = lax.all_gather(g_in, ("seq", "replica"))
+    g_in = g_in.reshape((n_seq, n_rep) + g_in.shape[1:])
+    g_in = jnp.transpose(g_in, (1, 3, 2, 0, 4)).reshape(kown, ranks, -1)
+    cutat = (0, wide, 2 * wide, 2 * wide + slim, 2 * wide + slim + heads)
+    g_in = jnp.concatenate(
+        [g_in[:, :, a:b].reshape(kown, -1) for a, b in zip(cutat, cutat[1:])], axis=1
+    ).astype(f32)
+    return (
+        block_out.reshape(tokens.shape),
+        grad_tokens.reshape(tokens.shape),
+        g_in,
+        g_out,
+        *smalls,
+    )
+
 
 def solution(mesh):
     in_specs = (
@@ -235,4 +460,6 @@
         P("shard"),
         P("shard"),
     )
-    return jax.shard_map(body, mesh=mesh, in_specs=in_specs, out_specs=out_specs, check_vma=False)
+    ranks = mesh.shape["shard"] * mesh.shape["seq"]
+    chosen = split_body if H % ranks == 0 and (INNER // ranks) % 128 == 0 else body
+    return jax.shard_map(chosen, mesh=mesh, in_specs=in_specs, out_specs=out_specs, check_vma=False)

time: 1750 us -> 1040 us (0.59)
  waiting for transfers between devices: 1310 us -> 401 us
  local copies, waits for them, and re-layouts: 68.4 us -> 199 us
  other arithmetic: 82.2 us -> 178 us
    reduce_scatter x2 -> x4, waiting for transfers between devices: 536 us -> 134 us  [the longest x1 62 us: split_body(): lax.psum_scatter(d_normed, TP, scatter_dimension=0, tiled=True).astype(f32)]
    psum x1, waiting for transfers between devices: 440 us -> 130 us  [split_body(): lax.psum((grad_pre, grad_cw, grad_cb, place(g_dtb, me * heads, H), place(...]
    all_gather x4, waiting for transfers between devices: 336 us -> 136 us  [the longest x1 84.8 us: split_body(): g_in = lax.all_gather(g_in, ('seq', 'replica'))]
    another operation x7 -> x30, other arithmetic: 4.9 us -> 82 us
    reshape x0 -> x33, local copies, waits for them, and re-layouts: none -> 50.1 us  [the longest x17 20.8 us: core(): p.reshape((seqs, length // span, span) + p.shape[2:])]
    unnamed x2 -> x1, blocking collectives: 14.2 us -> 60.3 us
    gather x0 -> x4, local copies, waits for them, and re-layouts: none -> 42.7 us  [the longest x3 41.1 us: split_body(): w_own = stack[order].reshape(n_shard * kown, -1)]
    psum x1 -> x2, blocking collectives: 65 us -> 25.5 us  [the longest x1 12.8 us: split_body(): total = lax.psum(jnp.sum(gated * gated, axis=-1), TP)]
  transfers between devices with their start and end apart: 10 -> 12, of which waited for: 7 -> 6; matrix products, arithmetic and copies ran while one was open for 13% -> 23% of each run, Pallas kernels for 0% -> 0%
where the time goes in v1:
time: 1040 us
  waiting for transfers between devices  401 us (39%)
  local copies, waits for them, and re-layouts  199 us (19%)
  other arithmetic  178 us (17%)
  matrix products  148 us (14%)
  blocking collectives  85.8 us (8%)
  between operations  18.1 us (2%)
    psum x1, waiting for transfers between devices, split_body(): lax.psum((grad_pre, grad_cw, grad_cb, place(g_dtb, me * heads, H), place(...  130 us
    all_gather x1, waiting for transfers between devices, split_body(): g_in = lax.all_gather(g_in, ('seq', 'replica'))  84.8 us
    another operation x27, other arithmetic  78.6 us
    reduce_scatter x1, waiting for transfers between devices, split_body(): lax.psum_scatter(d_normed, TP, scatter_dimension=0, tiled=True).astype(f32)  62 us
    unnamed x1, blocking collectives  60.3 us
    reduce_scatter x1, waiting for transfers between devices, split_body(): branch = lax.psum_scatter(branch, TP, scatter_dimension=0, tiled=True)  56.9 us
    dot_general x12, matrix products, span_local(): y_intra = jnp.einsum('stuh,suhp->sthp', kernel, values, precision=highest)  51.9 us
    all_gather x1, waiting for transfers between devices, split_body(): lax.all_gather(g_out, ('seq', 'replica'), axis=0, tiled=True).astype(f32)  51 us
  transfers between devices with their start and end apart: 12, of which 6 were waited for; matrix products, arithmetic and copies ran while one was open for 23% of the time, Pallas kernels for 0%

profile of v1, /device:TPU:0, one launch (start us, length us, event | category | flops | bytes accessed | tf_op | source)
XLA Modules:
  0.0 1035.7 jit_solution(8091096234435610607)
XLA Ops:
  17.6 60.3 %all-reduce.28 = bf16[21392]{0:T(1024)(128)(2,1)S(1)} all-reduce(bf16[21392]{0:T(1024)(128)(2,1)S(1)} %dynamic-update-slice), channel_id=2, replica_groups=mesh['seq'=4,'shard'=2,'replica'=4] {'shard'}, use_global_device_ids=true, to_apply=%add.28 | all-reduce | flops 21392 | bytes 85568
  85.8 21.2 %copy.466 = bf16[2,768,1030]{1,0,2:T(2,128)(2,1)} copy(bf16[2,768,1030]{1,2,0:T(8,128)(2,1)S(1)} %gather_fusion) | data formatting | bytes 6328320 | tf_op jit(solution)/shard_map/gather | solution.py:296
  107.0 8.5 reshape.585
  186.4 8.3 fusion.39
  239.4 12.8 %psum.63 = f32[2,1024]{1,0:T(2,128)} all-reduce(f32[2,1024]{1,0:T(2,128)} %get-tuple-element.82), channel_id=1, replica_groups=mesh['seq'=4,'shard'=2,'replica'=4] {'shard','seq'}, use_global_device_ids=true, to_apply=%region_10.11 | all-reduce | flops 2048 | bytes 16384 | tf_op jit(solution)/shard_map/psum | solution.py:336
  257.7 12.7 %psum.64 = f32[2,1024]{1,0:T(2,128)} all-reduce(f32[2,1024]{1,0:T(2,128)} %get-tuple-element.12), channel_id=1, replica_groups=mesh['seq'=4,'shard'=2,'replica'=4] {'shard','seq'}, use_global_device_ids=true, to_apply=%region_14.15 | all-reduce | flops 2048 | bytes 16384 | tf_op jit(solution)/shard_map/psum | solution.py:348
  271.1 8.5 multiply_reduce_fusion.1
  328.9 11.8 %fusion.56 = (f32[2,256,6]{1,2,0:T(8,128)}, f32[2,256,6]{1,2,0:T(8,128)}, f32[2,256,6]{1,2,0:T(8,128)}, f32[2,256,256]{2,1,0:T(8,128)}, f32[2,256,256]{2,1,0:T(8...) fusion(f32[2,256,6]{1,2,0:T(8,128)S(1)} %copy-done.146, ...), kind=kOutput, calls=%fused_computation.121 | convolution fusion | flops 644313088 | bytes 15613952 | tf_op jit(solution)/shard_map/transpose(jvp())/eval_jaxpr/stuh,suhp->sthp/dot_general | solution.py:74
  378.7 15.1 %reduce-window.70 = f32[2,6,2,128]{3,2,1,0:T(2,128)S(1)} reduce-window(f32[2,6,2,128]{3,2,1,0:T(2,128)S(1)} %reshape.623, f32[]{:T(128)} %constant.112.clone.1), window={size=1x1x1x128 pad=0_0x0_0x0_0x0_127}, to_apply=%region_36.37 | reduce-window | flops 390144 | bytes 24580 | tf_op jit(solution)/shard_map/reduce-window.10
  422.9 15.1 %reduce-window.66 = f32[2,6,2,128]{3,2,1,0:T(2,128)S(1)} reduce-window(f32[2,6,2,128]{3,2,1,0:T(2,128)S(1)} %reshape.622, f32[]{:T(128)} %constant.112.clone.1), window={size=1x1x1x128 pad=0_0x0_0x0_0x0_127}, to_apply=%region_29.30 | reduce-window | flops 390144 | bytes 24580 | tf_op jit(solution)/shard_map/reduce-window.8
  438.5 15.1 %reduce-window.76 = f32[2,6,2,128]{3,2,1,0:T(2,128)S(1)} reduce-window(f32[2,6,2,128]{3,2,1,0:T(2,128)S(1)} %reshape.625, f32[]{:T(128)} %constant.112.clone.1), window={size=1x1x1x128 pad=0_0x0_0x0_0x0_127}, to_apply=%region_50.51 | reduce-window | flops 390144 | bytes 24580 | tf_op jit(solution)/shard_map/reduce-window.14
  454.0 15.1 %reduce-window.74 = f32[2,6,2,128]{3,2,1,0:T(2,128)S(1)} reduce-window(f32[2,6,2,128]{3,2,1,0:T(2,128)S(1)} %reshape.624, f32[]{:T(128)} %constant.112.clone.1), window={size=1x1x1x128 pad=0_0x0_0x0_0x0_127}, to_apply=%region_43.44 | reduce-window | flops 390144 | bytes 24580 | tf_op jit(solution)/shard_map/reduce-window.12
  476.9 9.8 multiply_reduce_fusion.4
  498.3 10.2 convolution_convert_fusion.2
  513.4 17.3 %copy.641 = bf16[2,768,1030]{1,0,2:T(2,128)(2,1)S(1)} copy(bf16[2,768,1030]{1,2,0:T(8,128)(2,1)S(1)} %copy-done.7) | data formatting | bytes 6328320 | tf_op jit(solution)/shard_map/gather | solution.py:296
  536.0 8.6 convolution_convert_fusion.1
  556.1 14.8 %reduce-scatter.12.cloned.1.call-done = bf16[2,192,806]{2,1,0:T(8,128)(2,1)} async-done(((bf16[2,768,806]{2,1,0:T(8,128)(2,1)}), bf16[2,192,806]{2,1,0:T(8,128)(2,1)}) %reduce-scatter.12.cloned.1.call-update) | async-done | bytes 619024 | tf_op jit(solution)/shard_map/reduce_scatter | solution.py:412
  574.2 62.0 %reduce-scatter.10.cloned.1.call-done = bf16[256,1536]{1,0:T(8,128)(2,1)} async-done(((bf16[2048,1536]{1,0:T(8,128)(2,1)}), bf16[256,1536]{1,0:T(8,128)(2,1)}) %reduce-scatter.10.cloned.1.call-update) | async-done | bytes 786448 | tf_op jit(solution)/shard_map/reduce_scatter | solution.py:372
  640.4 51.0 %all-gather.9.cloned.1.call-done = bf16[1536,1536]{1,0:T(8,128)(2,1)} async-done(((bf16[96,1536]{1,0:T(8,128)(2,1)}), bf16[1536,1536]{1,0:T(8,128)(2,1)}) %all-gather.9.cloned.1.call-update) | async-done | bytes 4718608 | tf_op jit(solution)/shard_map/all_gather | solution.py:410
  698.8 56.9 %reduce-scatter.8.cloned.1.call-done = bf16[256,1536]{1,0:T(8,128)(2,1)} async-done(((bf16[2048,1536]{1,0:T(8,128)(2,1)}), bf16[256,1536]{1,0:T(8,128)(2,1)}) %reduce-scatter.8.cloned.1.call-update) | async-done | bytes 786448 | tf_op jit(solution)/shard_map/reduce_scatter | solution.py:340
  759.1 129.9 %all-reduce.32.cloned.1.call-done = (f32[1536]{0:T(1024)}, f32[4,3328]{1,0:T(4,128)}, f32[3328]{0:T(1024)}, f32[48]{0:T(128)}, f32[48]{0:T(128)}, /*index=5*/f32[48]{0:T(128)}, f32[3072]{0:T(1024)}) async-done(((f32[1536]{0:T(1024)}, f32[4,3328]{1,0:T(4,128)}, f32[3328]{0:T(1024)}, f32[48]{0:T(128)}, f32[48]{0:T(128)}, /*index=5*/f32[48]{0:T(128)}, f32[3072]{0:T(1024)}), (f32[1536]{0:T(1024)}, ...) | async-done | bytes 85584 | tf_op jit(solution)/shard_map/psum | solution.py:392
  898.2 84.8 %all-gather.15.cloned.1.call-done = bf16[32,192,806]{2,1,0:T(8,128)(2,1)} async-done(((bf16[2,192,806]{2,1,0:T(8,128)(2,1)}), bf16[32,192,806]{2,1,0:T(8,128)(2,1)}) %all-gather.15.cloned.1.call-update) | async-done | bytes 9904144 | tf_op jit(solution)/shard_map/all_gather | solution.py:420
  993.8 8.6 fusion.373
  1017.1 11.6 %maximum_convert_fusion = f32[768,6448]{0,1:T(8,128)} fusion(bf16[768,48]{0,1:T(8,128)(2,1)S(1)} %reshape.554, bf16[768,256]{0,1:T(8,128)(2,1)S(1)} %bitcast.761, bf16[768,3072]{0,1:T(8,128)(2,1)} %bitcast.748, bf16[768,3072]{0,1:T(8,128)(2,1)} %bitcast.747), kind=kLoop, calls=%fused_computation.7 | loop fusion | flops 39616512 | bytes 29712384 | tf_op jit(solution)/shard_map/convert_element_type | solution.py:426
  (717 shorter events, 347.8 us)
Async XLA Ops:
  7.2 108.4 %all-gather.11.cloned.1.call-start = ((), (), s32[]{:S(2)}) async-start(), calls=%async_computation.10 | async-start | bytes 7077888 | tf_op jit(solution)/shard_map/all_gather | solution.py:272
  7.9 143.1 %all-gather.13.cloned.1.call-start = ((), (), s32[]{:S(2)}) async-start(), calls=%async_computation.11 | async-start | bytes 7077888 | tf_op jit(solution)/shard_map/all_gather | solution.py:273
  8.7 487.6 %reduce-scatter.16.cloned.1.call-start = ((), (), s32[]{:S(2)}) async-start(), calls=%async_computation.13 | async-start | bytes 2359296
  12.7 68.4 %collective-permute-start = (bf16[768,1030]{0,1:T(8,128)(2,1)}, bf16[768,1030]{0,1:T(8,128)(2,1)S(1)}, u32[]{:S(2)}, u32[]{:S(2)}) collective-permute-start(bf16[768,1030]{0,1:T(8,128)(2,1)} %get-tuple-element.115), channel_id=1, source_target_pairs={{0,4},{4,0},{1,5},{5,1},{2,6},{6,2},{3,7},{7,3},{8,12},{12,8},{9,1... | collective-permute-start | bytes 4746248 | tf_op jit(solution)/shard_map/ppermute | solution.py:292
  78.6 84.5 %copy-start.181 = (f32[6]{0:T(128)}, f32[6]{0:T(128)S(1)}, u32[]{:S(2)}) copy-start(f32[6]{0:T(128)S(1)} %dynamic_slice.77) | copy-start | bytes 76
  80.3 106.0 %copy-start.120 = (f32[384]{0:T(512)}, f32[384]{0:T(512)S(1)}, u32[]{:S(2)}) copy-start(f32[384]{0:T(512)S(1)} %get-tuple-element.65) | copy-start | bytes 4612
  80.4 106.0 %copy-start.122 = (f32[384]{0:T(512)}, f32[384]{0:T(512)S(1)}, u32[]{:S(2)}) copy-start(f32[384]{0:T(512)S(1)} %get-tuple-element.66) | copy-start | bytes 4612
  80.4 106.0 %copy-start.124 = (f32[384]{0:T(512)}, f32[384]{0:T(512)S(1)}, u32[]{:S(2)}) copy-start(f32[384]{0:T(512)S(1)} %get-tuple-element.67) | copy-start | bytes 4612
  80.4 106.0 %copy-start.126 = (f32[384]{0:T(512)}, f32[384]{0:T(512)S(1)}, u32[]{:S(2)}) copy-start(f32[384]{0:T(512)S(1)} %get-tuple-element.68) | copy-start | bytes 4612
  406.2 138.6 %reduce-scatter.14.cloned.1.call-start = ((), (), s32[]{:S(2)}) async-start(), calls=%async_computation.8 | async-start | bytes 1474560 | tf_op jit(solution)/shard_map/reduce_scatter | solution.py:409
  486.7 84.2 %reduce-scatter.12.cloned.1.call-start = ((), (), s32[]{:S(2)}) async-start(), calls=%async_computation.7 | async-start | bytes 3440640 | tf_op jit(solution)/shard_map/reduce_scatter | solution.py:412
  513.1 123.0 %reduce-scatter.10.cloned.1.call-start = ((), (), s32[]{:S(2)}) async-start(), calls=%async_computation.6 | async-start | bytes 7077888 | tf_op jit(solution)/shard_map/reduce_scatter | solution.py:372
  544.7 146.8 %all-gather.9.cloned.1.call-start = ((), (), s32[]{:S(2)}) async-start(), calls=%async_computation.9 | async-start | bytes 5013504 | tf_op jit(solution)/shard_map/all_gather | solution.py:410
  545.4 210.3 %reduce-scatter.8.cloned.1.call-start = ((), (), s32[]{:S(2)}) async-start(), calls=%async_computation.5 | async-start | bytes 7077888 | tf_op jit(solution)/shard_map/reduce_scatter | solution.py:340
  552.6 83.5 %copy-start.98 = (f32[1536]{0:T(1024)S(1)}, f32[1536]{0:T(1024)}, u32[]{:S(2)}) copy-start(f32[1536]{0:T(1024)} %copy-done.97) | copy-start | bytes 18436
  552.7 336.4 %all-reduce.32.cloned.1.call-start = ((), (), s32[]{:S(2)}) async-start(), calls=%async_computation.14 | async-start | bytes 183296 | tf_op jit(solution)/shard_map/psum | solution.py:392
  554.4 84.0 %copy-start.110 = (f32[3072]{0:T(1024)}, f32[3072]{0:T(1024)S(1)}, u32[]{:S(2)}) copy-start(f32[3072]{0:T(1024)S(1)} %dynamic_update_slice.23) | copy-start | bytes 36868
  554.7 83.6 %copy-start.190 = (f32[48]{0:T(128)}, f32[48]{0:T(128)S(1)}, u32[]{:S(2)}) copy-start(f32[48]{0:T(128)S(1)} %dynamic_update_slice.22) | copy-start | bytes 580
  555.2 83.1 %copy-start.191 = (f32[48]{0:T(128)}, f32[48]{0:T(128)S(1)}, u32[]{:S(2)}) copy-start(f32[48]{0:T(128)S(1)} %dynamic_update_slice.20) | copy-start | bytes 580
  555.5 82.8 %copy-start.189 = (f32[48]{0:T(128)}, f32[48]{0:T(128)S(1)}, u32[]{:S(2)}) copy-start(f32[48]{0:T(128)S(1)} %multiply_dynamic-update-slice_fusion) | copy-start | bytes 580
  572.0 66.6 %collective-permute-start.1 = (bf16[192,806]{1,0:T(8,128)(2,1)S(1)}, bf16[192,806]{1,0:T(8,128)(2,1)S(1)}, u32[]{:S(2)}, u32[]{:S(2)}) collective-permute-start(bf16[192,806]{1,0:T(8,128)(2,1)S(1)} %get-tuple-element.113), channel_id=1, source_target_pairs={{0,4},{4,0},{1,5},{5,1},{2,6},{6,2},{3,7},{7,3},{8,12},{12,8},{9,1... | collective-permute-start | bytes 928520 | tf_op jit(solution)/shard_map/ppermute | solution.py:417
  638.4 344.6 %all-gather.15.cloned.1.call-start = ((), (), s32[]{:S(2)}) async-start(), calls=%async_computation.12 | async-start | bytes 11698176 | tf_op jit(solution)/shard_map/all_gather | solution.py:420
  640.4 115.3 %copy-start.26 = (bf16[1,256,1536]{2,1,0:T(8,128)(2,1)S(1)}, bf16[1,256,1536]{2,1,0:T(8,128)(2,1)}, u32[]{:S(2)}) copy-start(bf16[1,256,1536]{2,1,0:T(8,128)(2,1)} %param.21) | copy-start | bytes 2359300
  640.4 115.3 %copy-start.27 = (bf16[256,1536]{1,0:T(8,128)(2,1)S(1)}, bf16[256,1536]{1,0:T(8,128)(2,1)}, u32[]{:S(2)}) copy-start(bf16[256,1536]{1,0:T(8,128)(2,1)} %reduce-scatter.10.cloned.1.call-done) | copy-start | bytes 2359300
  (185 other events, 1579.3 us)
Sparse Core Ops, SparseCore 0:
  9.9 68.3 all-gather.10
  80.1 47.1 all-gather.12
  406.3 40.6 reduce-scatter.15
  486.8 28.9 reduce-scatter.13
  518.0 52.8 reduce-scatter.11
  574.7 61.3 reduce-scatter.9
  638.4 52.9 all-gather.8
  695.4 60.2 reduce-scatter.7
  763.3 125.7 all-reduce.31
  891.2 91.6 all-gather.14
